TPU v7x, 32 devices: a whole 2x2x4 slice. The times are simulated.
32 devices in a mesh: layer: 4 (over x, core), harm: 8 (over z, y).
Axes of the slice: x: 2, y: 2, z: 4, core: 2. Of those that a mesh axis runs over, the one named last changes fastest.
Arguments:
- source: bfloat16 [2, 2048, 128], P(None, 'harm'), may hold values from -6 to 6
- transfer: bfloat16 [4, 2, 2048, 2048], P('layer', None, 'harm'), may hold values from -0.09375 to 0.09375
- fields: bfloat16 [4, 2, 2048, 128], P('layer', None, 'harm'), may hold values from -6 to 6
- orders: int32 [2048], replicated, may hold values from 0 to 2047, each once
Outputs:
- gradients: float32 [4, 2, 4096], P('layer', None, 'harm')
- boundary: bfloat16 [4, 2, 2048, 128], P('layer', None, 'harm')
Inputs may be any that keep to these rules, and one draw needn't show every extreme that they name: `orders`: every value from 0 to 2047 appears exactly once.
All inputs are finite; a program needn't handle non-finite values.
Results may differ from a plain program's by a relative error of at most 0.006.
Values may be sent and summed in bfloat16 or wider, within the bound.
A program may use at most 64 MiB of HBM per device.

v0:
```python
import functools
import math

import jax
import jax.numpy as jnp
from jax import lax
from jax.experimental import pallas as pl
from jax.experimental.pallas import tpu as pltpu
from jax.sharding import PartitionSpec as P

MESH = pl.DeviceIdType.MESH
REACH = 3
CROSS = (0,)
FAR_FIRST = False


def flipped(index, bits, count):
    total = 0
    place = 1
    while place < count:
        digit = (index // place) % 2
        total = total + (1 - digit if (bits // place) % 2 else digit) * place
        place *= 2
    return total


def guarded(condition, action):
    if condition is None:
        action()
    else:
        pl.when(condition)(action)


def sweep_kernel(
    sections,
    members,
    inner,
    block,
    source_ref,
    transfer_ref,
    fields_ref,
    orders_ref,
    grads_ref,
    bottom_ref,
    matrix,
    staged,
    adj,
    fwd,
    out_block,
    onehot_adj,
    onehot_fwd,
    left,
    padded,
    local_sems,
    go_sem,
    adj_recv,
    adj_send,
    adj_relay,
    adj_forward,
    down_send,
    fwd_recv,
    fwd_send,
    fwd_relay,
    fwd_forward,
):
    outer = members // inner
    section = lax.axis_index("layer")
    member = lax.axis_index("harm")
    o_index, i_index = member // inner, member % inner
    rows = out_block.shape[0]
    harmonics = adj.shape[0]
    columns = adj.shape[1] // 2
    chunks = adj_recv.shape[0]
    lanes = adj.shape[1] // chunks
    half = lanes // 2
    band = 2 * harmonics // members
    width = block + band
    top = section == sections - 1
    early = section < sections // 2
    reach = min(REACH, outer - 1)
    near = sorted(range(1 - outer, outer), key=abs)
    order = sorted(range(-reach, reach + 1), key=abs, reverse=FAR_FIRST)

    def rows_of(index):
        return pl.ds(pl.multiple_of(index * rows, rows), rows)

    load_matrix = pltpu.make_async_copy(transfer_ref.at[0], matrix, local_sems.at[0])
    load_source = pltpu.make_async_copy(source_ref, staged, local_sems.at[1])
    load_fields = [
        pltpu.make_async_copy(
            fields_ref.at[0, part], fwd.at[rows_of(member), pl.ds(part * columns, columns)], local_sems.at[2 + part]
        )
        for part in range(2)
    ]
    load_source.start()
    load_matrix.start()
    for load in load_fields:
        load.start()

    barrier = pltpu.get_barrier_semaphore()
    peers = [(section, flipped(member, t, members)) for t in range(1, members)]
    for step in (1, sections - 1):
        peers += [((section + step) % sections, flipped(member, t, members)) for t in range(members)]
    for peer in peers:
        pl.semaphore_signal(barrier, inc=1, device_id=peer, device_id_type=MESH)
    load_source.wait()

    @pl.when(top)
    def _():
        for m in range(chunks):
            span = slice(m * half, (m + 1) * half)
            adj[rows_of(member), m * lanes : (m + 1) * lanes] = jnp.concatenate(
                [staged[0][:, span], staged[1][:, span]], axis=1
            )

    pl.semaphore_wait(barrier, len(peers))

    def present(d):
        return None if d == 0 else jnp.logical_and(o_index + d >= 0, o_index + d < outer)

    def lanes_of(buffer, recv, m):
        size = buffer.shape[1] // recv.shape[0]
        return pl.ds(m * size, size)

    def line_copy(buffer, send, recv, m, d, u, own_section=True):
        span = lanes_of(buffer, recv, m)
        return pltpu.make_async_remote_copy(
            src_ref=buffer.at[rows_of(member), span] if own_section else out_block.at[:, span],
            dst_ref=buffer.at[rows_of(member), span],
            send_sem=send.at[m, d + reach, u],
            recv_sem=recv.at[m, member],
            device_id=(section if own_section else section - 1, (o_index + d) * inner + flipped(i_index, u, inner)),
            device_id_type=MESH,
        )

    def forward_copy(buffer, send, recv, m, d, u):
        span = lanes_of(buffer, recv, m)
        held = member - d * inner
        return pltpu.make_async_remote_copy(
            src_ref=buffer.at[rows_of(held), span],
            dst_ref=buffer.at[rows_of(held), span],
            send_sem=send.at[m, d + outer - 1, u],
            recv_sem=recv.at[m, held],
            device_id=(section, o_index * inner + flipped(i_index, u, inner)),
            device_id_type=MESH,
        )

    def relay_copy(buffer, send, recv, m, d):
        span = lanes_of(buffer, recv, m)
        held = member - d * inner
        return pltpu.make_async_remote_copy(
            src_ref=buffer.at[rows_of(held), span],
            dst_ref=buffer.at[rows_of(held), span],
            send_sem=send.at[m, d + outer - 1],
            recv_sem=recv.at[m, held],
            device_id=(section, member + (inner if d > 0 else -inner)),
            device_id_type=MESH,
        )

    def relays(d):
        return reach <= abs(d) < outer - 1

    def onward(d):
        step = 1 if d > 0 else -1
        return jnp.logical_and(o_index + step >= 0, o_index + step < outer)

    def arrival(buffer, recv, m, index):
        span = lanes_of(buffer, recv, m)
        return pltpu.make_async_remote_copy(
            src_ref=buffer.at[rows_of(index), span],
            dst_ref=buffer.at[rows_of(index), span],
            send_sem=recv.at[m, index],
            recv_sem=recv.at[m, index],
            device_id=(section, index),
            device_id_type=MESH,
        )

    def each_line(buffer, send, recv, m, finish=False, own_section=True):
        for d in order:
            for u in range(inner if abs(d) in CROSS else 1):
                if own_section and d == 0 and u == 0:
                    continue
                copy = line_copy(buffer, send, recv, m, d, u, own_section)
                guarded(present(d), copy.wait_send if finish else copy.start)

    def each_down(m, finish=False):
        each_line(adj, down_send, adj_recv, m, finish, own_section=False)

    def pass_on(buffer, recv, relay, forward, m, d, finish=False):
        if relays(d):
            copy = relay_copy(buffer, relay, recv, m, d)
            guarded(onward(d), copy.wait_send if finish else copy.start)
        for u in range(1, inner if abs(d) not in CROSS else 1):
            copy = forward_copy(buffer, forward, recv, m, d, u)
            if finish:
                copy.wait_send()
            else:
                copy.start()

    def collect_line(buffer, recv, relay, forward, m, own_here):
        for d in near:

            def step(d=d):
                if d == 0 and own_here is None:
                    pass
                elif d == 0:
                    pl.when(jnp.logical_not(own_here))(arrival(buffer, recv, m, member).wait_recv)
                else:
                    arrival(buffer, recv, m, member - d * inner).wait_recv()
                pass_on(buffer, recv, relay, forward, m, d)

            guarded(present(-d), step)

    def collect_inner(buffer, recv, m):
        for t in range(outer):
            for u in range(1, inner):
                held = flipped(o_index, t, outer) * inner + flipped(i_index, u, inner)
                arrival(buffer, recv, m, held).wait_recv()

    def finish_passing(buffer, recv, relay, forward, m):
        for d in near:
            guarded(present(-d), functools.partial(pass_on, buffer, recv, relay, forward, m, d, finish=True))

    def start_fields():
        for m in range(fwd_recv.shape[0]):
            each_line(fwd, fwd_send, fwd_recv, m)

    def relay_fields():
        for m in range(fwd_recv.shape[0]):
            collect_line(fwd, fwd_recv, fwd_relay, fwd_forward, m, None)

    def finish_fields():
        for m in range(fwd_recv.shape[0]):
            collect_inner(fwd, fwd_recv, m)

    def build_onehots():
        @pl.loop(0, harmonics // block)
        def _(index):
            start = pl.multiple_of(index * block, block)
            line = lax.broadcasted_iota(jnp.int32, (block, harmonics), 0)
            orders = orders_ref[...].reshape(1, harmonics) - start
            dtype = onehot_adj.dtype
            onehot_adj[pl.ds(start, block), :] = jnp.where(orders == line, 1.0, 0.0).astype(dtype)
            onehot_fwd[pl.ds(start, block), :] = jnp.where(orders == block - 1 - line, 1.0, 0.0).astype(dtype)

        padded[:harmonics, :] = jnp.zeros((harmonics, 2 * columns), padded.dtype)
        padded[2 * harmonics :, :] = jnp.zeros((harmonics, 2 * columns), padded.dtype)

    def sort_fields():
        @pl.loop(0, harmonics // block)
        def _(index):
            start = pl.multiple_of(index * block, block)
            sorted_rows = jnp.dot(onehot_fwd[pl.ds(start, block), :], fwd[...], preferred_element_type=jnp.float32)
            real, imag = sorted_rows[:, :columns], sorted_rows[:, columns:]
            for_real, for_imag = [], []
            for m in range(chunks):
                span = slice(m * half, (m + 1) * half)
                for_real += [real[:, span], -imag[:, span]]
                for_imag += [imag[:, span], real[:, span]]
            left[index, :block, :] = jnp.concatenate(for_real, axis=1).astype(left.dtype)
            left[index, block:, :] = jnp.concatenate(for_imag, axis=1).astype(left.dtype)

    tile = 2 * block if harmonics % (2 * block) == 0 else block

    def sort_adjoint():
        @pl.loop(0, harmonics // tile)
        def _(index):
            start = pl.multiple_of(index * tile, tile)
            padded[pl.ds(pl.multiple_of(harmonics + start, tile), tile), :] = jnp.dot(
                onehot_adj[pl.ds(start, tile), :], adj[...], preferred_element_type=jnp.float32
            ).astype(padded.dtype)

    @pl.when(top)
    def _():
        for m in range(chunks):
            each_line(adj, adj_send, adj_recv, m)

    for load in load_fields:
        load.wait()

    @pl.when(jnp.logical_not(early) & jnp.logical_not(top))
    def _():
        build_onehots()

    @pl.when(section < sections // 2 - 1)
    def _():
        build_onehots()
        pl.semaphore_wait(go_sem, 1)

    @pl.when(early)
    def _():
        start_fields()

    @pl.when(section == sections // 2 - 1)
    def _():
        build_onehots()

    @pl.when(early)
    def _():
        relay_fields()
        finish_fields()

    @pl.when(early & (section > 0))
    def _():
        pl.semaphore_signal(go_sem, inc=1, device_id=(section - 1, member), device_id_type=MESH)

    @pl.when(early)
    def _():
        sort_fields()

    load_matrix.wait()
    for m in range(chunks):
        collect_line(adj, adj_recv, adj_relay, adj_forward, m, top)
    results = []
    for m in range(chunks):
        collect_inner(adj, adj_recv, m)
        values = adj[:, m * lanes : (m + 1) * lanes]
        by_real = jnp.dot(matrix[0], values, preferred_element_type=jnp.float32)
        by_imag = jnp.dot(matrix[1], values, preferred_element_type=jnp.float32)
        real = by_real[:, :half] - by_imag[:, half:]
        imag = by_real[:, half:] + by_imag[:, :half]
        out_block[:, m * lanes : (m + 1) * lanes] = jnp.concatenate([real, imag], axis=1).astype(out_block.dtype)

        @pl.when(section > 0)
        def _(m=m):
            each_down(m)

    for part in range(2):
        pieces = [out_block[:, m * lanes + part * half : m * lanes + (part + 1) * half] for m in range(chunks)]
        bottom_ref[part] = jnp.concatenate(pieces, axis=1)


    @pl.when(top)
    def _():
        build_onehots()


    @pl.when(jnp.logical_not(early))
    def _():
        start_fields()
        relay_fields()
        sort_adjoint()
        finish_fields()
        sort_fields()

    @pl.when(early)
    def _():
        sort_adjoint()

    total = jnp.zeros((2 * block, width), jnp.float32)
    for index in range(harmonics // block):
        window = padded[pl.ds(pl.multiple_of(member * band + index * block, block), width), :]
        total = total + lax.dot_general(
            left[index], window, (((1,), (1,)), ((), ())), preferred_element_type=jnp.float32
        )
    for part in range(2):
        rolled = pltpu.roll(
            total[part * block : (part + 1) * block], width - block, 1, stride=1, stride_axis=0
        )
        grads_ref[part : part + 1, :] = jnp.sum(rolled, axis=0, keepdims=True)[:, :band]

    for m in range(chunks):
        finish_passing(adj, adj_recv, adj_relay, adj_forward, m)
    for m in range(fwd_recv.shape[0]):
        each_line(fwd, fwd_send, fwd_recv, m, finish=True)
        finish_passing(fwd, fwd_recv, fwd_relay, fwd_forward, m)

    @pl.when(top)
    def _():
        for m in range(chunks):
            each_line(adj, adj_send, adj_recv, m, finish=True)

    @pl.when(section > 0)
    def _():
        for m in range(chunks):
            each_down(m, finish=True)


def per_device(source, transfer, fields, orders):
    harmonics = orders.shape[0]
    sections = lax.axis_size("layer")
    members = lax.axis_size("harm")
    rows = transfer.shape[2]
    columns = source.shape[2]
    inner = 1 << ((members.bit_length() - 1) // 2)
    outer = members // inner
    band = 2 * harmonics // members
    block = min(128, band)
    chunks = max(1, 2 * columns // 128)
    reach = min(REACH, outer - 1)
    norm_scale = 1.0 / math.sqrt(harmonics * columns)
    any_space = pl.BlockSpec(memory_space=pl.ANY)
    vmem = pl.BlockSpec(memory_space=pltpu.VMEM)
    dma = pltpu.SemaphoreType.DMA
    grads, bottom = pl.pallas_call(
        functools.partial(sweep_kernel, sections, members, inner, block),
        out_shape=(
            jax.ShapeDtypeStruct((2, band), jnp.float32),
            jax.ShapeDtypeStruct((2, rows, columns), jnp.bfloat16),
        ),
        in_specs=[any_space, any_space, any_space, vmem],
        out_specs=(vmem, vmem),
        scratch_shapes=[
            pltpu.VMEM((2, rows, harmonics), jnp.bfloat16),
            pltpu.VMEM((2, rows, columns), jnp.bfloat16),
            pltpu.VMEM((harmonics, 2 * columns), jnp.bfloat16),
            pltpu.VMEM((harmonics, 2 * columns), jnp.bfloat16),
            pltpu.VMEM((rows, 2 * columns), jnp.bfloat16),
            pltpu.VMEM((harmonics, harmonics), jnp.bfloat16),
            pltpu.VMEM((harmonics, harmonics), jnp.bfloat16),
            pltpu.VMEM((harmonics // block, 2 * block, 2 * columns), jnp.bfloat16),
            pltpu.VMEM((3 * harmonics, 2 * columns), jnp.bfloat16),
            dma((4,)),
            pltpu.SemaphoreType.REGULAR,
            dma((chunks, members)),
            dma((chunks, 2 * reach + 1, inner)),
            dma((chunks, 2 * outer - 1)),
            dma((chunks, 2 * outer - 1, inner)),
            dma((chunks, 2 * reach + 1, inner)),
            dma((1, members)),
            dma((1, 2 * reach + 1, inner)),
            dma((1, 2 * outer - 1)),
            dma((1, 2 * outer - 1, inner)),
        ],
        compiler_params=pltpu.CompilerParams(collective_id=0, has_side_effects=True),
        name="sweep",
    )(source, transfer, fields, orders)
    return (grads * norm_scale)[None], bottom[None]


def solution(mesh):
    return jax.shard_map(
        per_device,
        mesh=mesh,
        in_specs=(
            P(None, "harm", None),
            P("layer", None, "harm", None),
            P("layer", None, "harm", None),
            P(),
        ),
        out_specs=(P("layer", None, "harm"), P("layer", None, "harm", None)),
        check_vma=False,
    )
```

profile of v0, /device:TPU:0, one launch (start us, length us, event | category | flops | bytes accessed | tf_op | source)
XLA Modules:
  0.0 59.9 jit_solution(10712086231512653990)
XLA Ops:
  0.6 56.4 %sweep.1 = (f32[2,512]{1,0:T(2,128)}, bf16[2,256,128]{2,1,0:T(8,128)(2,1)}) custom-call(bf16[2,256,128]{2,1,0:T(8,128)(2,1)} %source_ref.1, bf16[1,2,256,2048]{3,2,1,0:T(8,128)(2,1)} %transfer_ref.1, bf16[1,2,256,128]{3,2,1,0:T(8,128)(2,1)} %fields_ref.1, s32[2048]{0:T(1024)} %orders_ref.1), custom_call_target="tpu_custom_call" | custom-call | tf_op jit(solution)/shard_map/sweep/pallas_call | solution.py:395
  57.0 1.3 %multiply_bitcast_fusion = f32[1,2,512]{2,1,0:T(2,128)} fusion(f32[2,512]{1,0:T(2,128)} %get-tuple-element.4), kind=kLoop, calls=%fused_computation | loop fusion | flops 1024 | bytes 8192 | tf_op jit(solution)/shard_map/broadcast_in_dim | solution.py:428
  58.3 1.6 %copy.7 = bf16[1,2,256,128]{3,2,1,0:T(8,128)(2,1)} copy(bf16[1,2,256,128]{3,2,1,0:T(8,128)(2,1)} %bitcast.3) | data formatting | bytes 262144
where the time goes:
time: 60.1 us; the launch traced here: 59.9 us
  Pallas kernels  56.4 us (94%)
  local copies, waits for them, and re-layouts  1.57 us (3%)
  other arithmetic  1.28 us (2%)
  between operations  0.64 us (1%)
    pallas_call x1, Pallas kernels, per_device(): pl.pallas_call(functools.partial(sweep_kernel, sections, members, inner,...  56.4 us
    unnamed x1, local copies, waits for them, and re-layouts  1.57 us
    broadcast_in_dim x1, other arithmetic, per_device(): return ((grads * norm_scale)[None], bottom[None])  1.28 us

commit v1 on v0

v1 whole, which is shorter than its diff:
```python
import contextlib
import functools
import math

import jax
import jax.numpy as jnp
from jax import lax
from jax.experimental import pallas as pl
from jax.experimental.pallas import tpu as pltpu
from jax.sharding import PartitionSpec as P

MESH = pl.DeviceIdType.MESH
REACH = 3
CHUNKS = 4


def scope(name):
    return contextlib.nullcontext()


def flipped(index, bits, count):
    total = 0
    place = 1
    while place < count:
        digit = (index // place) % 2
        total = total + (1 - digit if (bits // place) % 2 else digit) * place
        place *= 2
    return total


def across(left_values, right_values):
    return lax.dot_general(
        left_values, right_values, (((1,), (1,)), ((), ())), preferred_element_type=jnp.float32
    )


def guarded(condition, action):
    if condition is None:
        action()
    else:
        pl.when(condition)(action)


def sweep_kernel(
    sections,
    members,
    inner,
    block,
    source_ref,
    transfer_ref,
    fields_ref,
    orders_ref,
    grads_ref,
    bottom_ref,
    matrix,
    staged,
    adj,
    fwd,
    out_block,
    onehot_adj,
    onehot_fwd,
    left,
    padded,
    local_sems,
    go_sem,
    adj_recv,
    adj_send,
    adj_relay,
    adj_forward,
    down_send,
    fwd_recv,
    fwd_send,
    fwd_relay,
    fwd_forward,
):
    outer = members // inner
    section = lax.axis_index("layer")
    member = lax.axis_index("harm")
    o_index, i_index = member // inner, member % inner
    columns, rows = out_block.shape[1:]
    harmonics = members * rows
    chunks = adj_recv.shape[0]
    span = columns // chunks
    band = 2 * harmonics // members
    width = block + band
    top = section == sections - 1
    early = section < sections // 2
    from_chip = section % 2 == 0
    reach = min(REACH, outer - 1)
    near = sorted(range(1 - outer, outer), key=abs)
    order = sorted(range(-reach, reach + 1), key=abs)
    aligned = rows % 128 == 0

    def rows_of(index):
        return pl.ds(pl.multiple_of(index * rows, rows), rows)

    def sources_of(m):
        return pl.ds(m * span, span)

    load_matrix = pltpu.make_async_copy(transfer_ref.at[0], matrix, local_sems.at[0])
    load_source = pltpu.make_async_copy(source_ref, staged, local_sems.at[1])
    load_fields = [
        pltpu.make_async_copy(
            fields_ref.at[0, part], fwd.at[rows_of(member), pl.ds(part * columns, columns)], local_sems.at[2 + part]
        )
        for part in range(2)
    ]
    load_source.start()
    load_matrix.start()
    for load in load_fields:
        load.start()

    barrier = pltpu.get_barrier_semaphore()
    peers = [(section, flipped(member, t, members)) for t in range(1, members)]
    for step in (1, sections - 1):
        peers += [((section + step) % sections, flipped(member, t, members)) for t in range(members)]
    for peer in peers:
        pl.semaphore_signal(barrier, inc=1, device_id=peer, device_id_type=MESH)
    load_source.wait()

    @pl.when(top)
    def _():
        for part in range(2):
            adj[member, part] = staged[part].T

    with scope("bar"):
        pl.semaphore_wait(barrier, len(peers))

    def present(d):
        return None if d == 0 else jnp.logical_and(o_index + d >= 0, o_index + d < outer)

    def adj_view(m, held):
        return adj.at[held, :, sources_of(m), :]

    def fwd_view(m, held):
        return fwd.at[rows_of(held), :]

    def send_view(m, held):
        return out_block.at[:, sources_of(m), :]

    def line_copy(view, send, recv, m, d, u, down=False):
        return pltpu.make_async_remote_copy(
            src_ref=send_view(m, member) if down else view(m, member),
            dst_ref=view(m, member),
            send_sem=send.at[m, d + reach, u],
            recv_sem=recv.at[m, member],
            device_id=(section - 1 if down else section, (o_index + d) * inner + flipped(i_index, u, inner)),
            device_id_type=MESH,
        )

    def forward_copy(view, send, recv, m, d, u):
        held = member - d * inner
        return pltpu.make_async_remote_copy(
            src_ref=view(m, held),
            dst_ref=view(m, held),
            send_sem=send.at[m, d + outer - 1, u],
            recv_sem=recv.at[m, held],
            device_id=(section, o_index * inner + flipped(i_index, u, inner)),
            device_id_type=MESH,
        )

    def relay_copy(view, send, recv, m, d):
        held = member - d * inner
        return pltpu.make_async_remote_copy(
            src_ref=view(m, held),
            dst_ref=view(m, held),
            send_sem=send.at[m, d + outer - 1],
            recv_sem=recv.at[m, held],
            device_id=(section, member + (inner if d > 0 else -inner)),
            device_id_type=MESH,
        )

    def relays(d):
        return reach <= abs(d) < outer - 1

    def onward(d):
        step = 1 if d > 0 else -1
        return jnp.logical_and(o_index + step >= 0, o_index + step < outer)

    def arrival(view, recv, m, index):
        return pltpu.make_async_remote_copy(
            src_ref=view(m, index),
            dst_ref=view(m, index),
            send_sem=recv.at[m, index],
            recv_sem=recv.at[m, index],
            device_id=(section, index),
            device_id_type=MESH,
        )

    def each_line(view, send, recv, m, finish=False, down=False):
        for d in order:
            for u in range(inner if d == 0 else 1):
                if not down and d == 0 and u == 0:
                    continue
                copy = line_copy(view, send, recv, m, d, u, down)
                condition = present(d)
                if down and d == 0 and u > 0:
                    condition = jnp.logical_not(from_chip)
                guarded(condition, copy.wait_send if finish else copy.start)

    def each_down(m, finish=False):
        each_line(adj_view, down_send, adj_recv, m, finish, down=True)

    def pass_on(view, recv, relay, forward, m, d, finish=False, cross_here=None):
        if relays(d):
            copy = relay_copy(view, relay, recv, m, d)
            guarded(onward(d), copy.wait_send if finish else copy.start)
        if d == 0 and cross_here is None:
            return
        for u in range(1, inner):
            copy = forward_copy(view, forward, recv, m, d, u)
            guarded(cross_here if d == 0 else None, copy.wait_send if finish else copy.start)

    def collect_line(view, recv, relay, forward, m, own_here, cross_here=None):
        for d in near:

            def step(d=d):
                if d == 0 and own_here is None:
                    pass
                elif d == 0:
                    pl.when(jnp.logical_not(own_here))(arrival(view, recv, m, member).wait_recv)
                else:
                    arrival(view, recv, m, member - d * inner).wait_recv()
                pass_on(view, recv, relay, forward, m, d, cross_here=cross_here)

            guarded(present(-d), step)

    def crossed(t, u):
        return flipped(o_index, t, outer) * inner + flipped(i_index, u, inner)

    def collect_inner(view, recv, m):
        for t in range(outer):
            for u in range(1, inner):
                arrival(view, recv, m, crossed(t, u)).wait_recv()

    def finish_passing(view, recv, relay, forward, m, cross_here=None):
        for d in near:
            guarded(
                present(-d),
                functools.partial(
                    pass_on, view, recv, relay, forward, m, d, finish=True, cross_here=cross_here
                ),
            )

    def start_fields():
        for m in range(fwd_recv.shape[0]):
            each_line(fwd_view, fwd_send, fwd_recv, m)

    def relay_fields():
        for m in range(fwd_recv.shape[0]):
            collect_line(fwd_view, fwd_recv, fwd_relay, fwd_forward, m, None)

    def finish_fields():
        for m in range(fwd_recv.shape[0]):
            collect_inner(fwd_view, fwd_recv, m)

    def build_onehots():
        @pl.loop(0, harmonics // block)
        def _(index):
            start = pl.multiple_of(index * block, block)
            line = lax.broadcasted_iota(jnp.int32, (block, harmonics), 0)
            orders = orders_ref[...].reshape(1, harmonics) - start
            dtype = onehot_adj.dtype
            onehot_adj[pl.ds(start, block), :] = jnp.where(orders == line, 1.0, 0.0).astype(dtype)
            onehot_fwd[pl.ds(start, block), :] = jnp.where(orders == block - 1 - line, 1.0, 0.0).astype(dtype)

        padded[:, :harmonics] = jnp.zeros((2 * columns, harmonics), padded.dtype)
        padded[:, 2 * harmonics :] = jnp.zeros((2 * columns, harmonics), padded.dtype)

    batch = math.gcd(4, harmonics // block)

    def sort_fields():
        @pl.loop(0, harmonics // (block * batch))
        def _(index):
            start = pl.multiple_of(index * block * batch, block * batch)
            sorted_rows = jnp.dot(
                onehot_fwd[pl.ds(start, block * batch), :], fwd[...], preferred_element_type=jnp.float32
            )
            for part in range(batch):
                piece = sorted_rows[part * block : (part + 1) * block]
                real, imag = piece[:, :columns], piece[:, columns:]
                at = index * batch + part
                left[at, :block, :] = jnp.concatenate([real, -imag], axis=1).astype(left.dtype)
                left[at, block:, :] = jnp.concatenate([imag, real], axis=1).astype(left.dtype)

    tile = math.gcd(512, harmonics)

    def sort_adjoint():
        @pl.loop(0, harmonics // tile)
        def _(index):
            start = pl.multiple_of(index * tile, tile)
            total = None
            for held in range(members):
                values = adj[held].reshape(2 * columns, rows)
                term = across(values, onehot_adj[pl.ds(start, tile), held * rows : (held + 1) * rows])
                total = term if total is None else total + term
            padded[:, pl.ds(pl.multiple_of(harmonics + start, tile), tile)] = total.astype(padded.dtype)

    @pl.when(top)
    def _():
        for m in range(chunks):
            each_line(adj_view, adj_send, adj_recv, m)

    for load in load_fields:
        load.wait()

    @pl.when(jnp.logical_not(early) & jnp.logical_not(top))
    def _():
        build_onehots()

    @pl.when(section < sections // 2 - 1)
    def _():
        build_onehots()
        pl.semaphore_wait(go_sem, 1)

    @pl.when(early)
    def _():
        start_fields()

    @pl.when(section == sections // 2 - 1)
    def _():
        build_onehots()

    @pl.when(early)
    def _():
        with scope("ef_relay"):
            relay_fields()
        with scope("ef_finish"):
            finish_fields()

    @pl.when(early & (section > 0))
    def _():
        pl.semaphore_signal(go_sem, inc=1, device_id=(section - 1, member), device_id_type=MESH)

    @pl.when(early)
    def _():
        with scope("ef_sort"):
            sort_fields()

    load_matrix.wait()
    cross_adj = jnp.logical_not(from_chip) & jnp.logical_not(top)
    partials = {}

    def terms(m, helds):
        total = None
        for held in helds:
            real, imag = adj[held, 0, sources_of(m), :], adj[held, 1, sources_of(m), :]
            here = rows_of(held) if aligned else slice(held * rows, (held + 1) * rows)
            for part, values in enumerate(([real, imag], [-imag, real])):
                term = across(jnp.concatenate(values, axis=0), matrix[part, :, here])
                total = term if total is None else total + term
        return total

    def line_step(m):
        with scope("line%d" % m):
            collect_line(adj_view, adj_recv, adj_relay, adj_forward, m, top, cross_adj)

    def first_step(m):
        if aligned:
            partials[m] = terms(m, [crossed(t, 0) for t in range(outer)])

    def last_step(m):
        with scope("inner%d" % m):
            collect_inner(adj_view, adj_recv, m)
        if aligned:
            total = partials[m] + terms(m, [crossed(t, u) for t in range(outer) for u in range(1, inner)])
        else:
            total = terms(m, range(members))
        for part in range(2):
            out_block[part, sources_of(m), :] = total[part * span : (part + 1) * span].astype(out_block.dtype)

        @pl.when(section > 0)
        def _():
            each_down(m)

    ahead = 2
    for m in range(chunks + ahead):
        if m < chunks:
            line_step(m)
        if m >= ahead:
            last_step(m - ahead)
        if m < chunks:
            first_step(m)

    for part in range(2):
        bottom_ref[part] = out_block[part].T

    @pl.when(top)
    def _():
        build_onehots()

    @pl.when(jnp.logical_not(early))
    def _():
        with scope("lf_relay"):
            start_fields()
            relay_fields()
        with scope("lsortadj"):
            sort_adjoint()
        with scope("lf_finish"):
            finish_fields()
        with scope("lf_sort"):
            sort_fields()

    @pl.when(early)
    def _():
        with scope("esortadj"):
            sort_adjoint()

    with scope("grad"):
        total = jnp.zeros((2 * block, width), jnp.float32)
        for index in range(harmonics // block):
            start = member * band + index * block
            if block % 128 == 0:
                window = padded[:, pl.ds(pl.multiple_of(start, block), width)]
            else:
                near_start = pl.multiple_of(start // 128 * 128, 128)
                wide = padded[:, pl.ds(near_start, (width + 255) // 128 * 128)]
                window = wide[:, :width]
                for shift in range(block, 128, block):
                    window = jnp.where(start - near_start == shift, wide[:, shift : shift + width], window)
            total = total + jnp.dot(left[index], window, preferred_element_type=jnp.float32)
        for part in range(2):
            rolled = pltpu.roll(
                total[part * block : (part + 1) * block], width - block, 1, stride=1, stride_axis=0
            )
            grads_ref[part : part + 1, :] = jnp.sum(rolled, axis=0, keepdims=True)[:, :band]

    with scope("fin"):
        for m in range(chunks):
            finish_passing(adj_view, adj_recv, adj_relay, adj_forward, m, cross_adj)
        for m in range(fwd_recv.shape[0]):
            each_line(fwd_view, fwd_send, fwd_recv, m, finish=True)
            finish_passing(fwd_view, fwd_recv, fwd_relay, fwd_forward, m)

        @pl.when(top)
        def _():
            for m in range(chunks):
                each_line(adj_view, adj_send, adj_recv, m, finish=True)

        @pl.when(section > 0)
        def _():
            for m in range(chunks):
                each_down(m, finish=True)


def per_device(source, transfer, fields, orders):
    harmonics = orders.shape[0]
    sections = lax.axis_size("layer")
    members = lax.axis_size("harm")
    rows = transfer.shape[2]
    columns = source.shape[2]
    inner = 1 << ((members.bit_length() - 1) // 2)
    outer = members // inner
    band = 2 * harmonics // members
    block = min(128, band)
    chunks = math.gcd(CHUNKS, columns)
    reach = min(REACH, outer - 1)
    norm_scale = 1.0 / math.sqrt(harmonics * columns)
    any_space = pl.BlockSpec(memory_space=pl.ANY)
    vmem = pl.BlockSpec(memory_space=pltpu.VMEM)
    dma = pltpu.SemaphoreType.DMA
    grads, bottom = pl.pallas_call(
        functools.partial(sweep_kernel, sections, members, inner, block),
        out_shape=(
            jax.ShapeDtypeStruct((2, band), jnp.float32),
            jax.ShapeDtypeStruct((2, rows, columns), jnp.bfloat16),
        ),
        in_specs=[any_space, any_space, any_space, vmem],
        out_specs=(vmem, vmem),
        scratch_shapes=[
            pltpu.VMEM((2, rows, harmonics), jnp.bfloat16),
            pltpu.VMEM((2, rows, columns), jnp.bfloat16),
            pltpu.VMEM((members, 2, columns, rows), jnp.bfloat16),
            pltpu.VMEM((harmonics, 2 * columns), jnp.bfloat16),
            pltpu.VMEM((2, columns, rows), jnp.bfloat16),
            pltpu.VMEM((harmonics, harmonics), jnp.bfloat16),
            pltpu.VMEM((harmonics, harmonics), jnp.bfloat16),
            pltpu.VMEM((harmonics // block, 2 * block, 2 * columns), jnp.bfloat16),
            pltpu.VMEM((2 * columns, 3 * harmonics), jnp.bfloat16),
            dma((4,)),
            pltpu.SemaphoreType.REGULAR,
            dma((chunks, members)),
            dma((chunks, 2 * reach + 1, inner)),
            dma((chunks, 2 * outer - 1)),
            dma((chunks, 2 * outer - 1, inner)),
            dma((chunks, 2 * reach + 1, inner)),
            dma((1, members)),
            dma((1, 2 * reach + 1, inner)),
            dma((1, 2 * outer - 1)),
            dma((1, 2 * outer - 1, inner)),
        ],
        compiler_params=pltpu.CompilerParams(collective_id=0, has_side_effects=True),
        name="sweep",
    )(source, transfer, fields, orders)
    return (grads * norm_scale)[None], bottom[None]


def solution(mesh):
    return jax.shard_map(
        per_device,
        mesh=mesh,
        in_specs=(
            P(None, "harm", None),
            P("layer", None, "harm", None),
            P("layer", None, "harm", None),
            P(),
        ),
        out_specs=(P("layer", None, "harm"), P("layer", None, "harm", None)),
        check_vma=False,
    )
```

time: 60.1 us -> 61 us (1.015)
  Pallas kernels: 56.4 us -> 57.3 us
    pallas_call x1, Pallas kernels: 56.4 us -> 57.3 us  [per_device(): pl.pallas_call(functools.partial(sweep_kernel, sections, members, inner,...]
where the time goes in v1:
time: 61 us; the launch traced here: 60.8 us
  Pallas kernels  57.3 us (94%)
  local copies, waits for them, and re-layouts  1.57 us (3%)
  other arithmetic  1.28 us (2%)
  between operations  0.64 us (1%)
    pallas_call x1, Pallas kernels, per_device(): pl.pallas_call(functools.partial(sweep_kernel, sections, members, inner,...  57.3 us
    unnamed x1, local copies, waits for them, and re-layouts  1.57 us
    broadcast_in_dim x1, other arithmetic, per_device(): return ((grads * norm_scale)[None], bottom[None])  1.28 us

profile of v1, /device:TPU:0, one launch (start us, length us, event | category | flops | bytes accessed | tf_op | source)
XLA Modules:
  0.0 60.8 jit_solution(738088774133600302)
XLA Ops:
  0.6 57.3 %sweep.1 = (f32[2,512]{1,0:T(2,128)}, bf16[2,256,128]{2,1,0:T(8,128)(2,1)}) custom-call(bf16[2,256,128]{2,1,0:T(8,128)(2,1)} %source_ref.1, bf16[1,2,256,2048]{3,2,1,0:T(8,128)(2,1)} %transfer_ref.1, bf16[1,2,256,128]{3,2,1,0:T(8,128)(2,1)} %fields_ref.1, s32[2048]{0:T(1024)} %orders_ref.1), custom_call_target="tpu_custom_call" | custom-call | tf_op jit(solution)/shard_map/sweep/pallas_call | solution.py:462
  57.9 1.3 %multiply_bitcast_fusion = f32[1,2,512]{2,1,0:T(2,128)} fusion(f32[2,512]{1,0:T(2,128)} %get-tuple-element.4), kind=kLoop, calls=%fused_computation | loop fusion | flops 1024 | bytes 8192 | tf_op jit(solution)/shard_map/broadcast_in_dim | solution.py:495
  59.2 1.6 %copy.7 = bf16[1,2,256,128]{3,2,1,0:T(8,128)(2,1)} copy(bf16[1,2,256,128]{3,2,1,0:T(8,128)(2,1)} %bitcast.3) | data formatting | bytes 262144

commit v2 on v1

v2 whole, which is shorter than its diff:
```python
import contextlib
import functools
import math

import jax
import jax.numpy as jnp
from jax import lax
from jax.experimental import pallas as pl
from jax.experimental.pallas import tpu as pltpu
from jax.sharding import PartitionSpec as P

MESH = pl.DeviceIdType.MESH
CHUNKS = 4
AHEAD = 2


def scope(name):
    return contextlib.nullcontext()


def flipped(index, bits, count):
    total = 0
    place = 1
    while place < count:
        digit = (index // place) % 2
        total = total + (1 - digit if (bits // place) % 2 else digit) * place
        place *= 2
    return total


def guarded(condition, action):
    if condition is None:
        action()
    else:
        pl.when(condition)(action)


def sweep_kernel(
    sections,
    members,
    inner,
    block,
    source_ref,
    transfer_ref,
    fields_ref,
    orders_ref,
    grads_ref,
    bottom_ref,
    matrix,
    turned,
    staged,
    adj,
    fwd,
    out_block,
    bottom,
    onehot_adj,
    onehot_fwd,
    left,
    padded,
    product,
    partial,
    arrived,
    local_sems,
    adj_recv,
    adj_send,
    adj_forward,
    down_send,
    fwd_recv,
    fwd_send,
    fwd_forward,
    sum_recv,
    sum_send,
):
    outer = members // inner
    section = lax.axis_index("layer")
    member = lax.axis_index("harm")
    o_index, i_index = member // inner, member % inner
    columns, rows = out_block.shape[1:]
    harmonics = members * rows
    chunks = adj_recv.shape[0]
    span = columns // chunks
    band = 2 * harmonics // members
    width = block + band
    top = section == sections - 1
    early = section < sections // 2
    crosses = section % 2 == 0

    def rows_of(index):
        return pl.ds(pl.multiple_of(index * rows, rows), rows)

    def sources_of(m):
        return pl.ds(m * span, span)

    def at(t, u):
        return flipped(o_index, t, outer) * inner + flipped(i_index, u, inner)

    load_matrix = pltpu.make_async_copy(transfer_ref.at[0], matrix, local_sems.at[0])
    load_source = pltpu.make_async_copy(source_ref, staged, local_sems.at[1])
    load_fields = [
        pltpu.make_async_copy(
            fields_ref.at[0, part], fwd.at[rows_of(member), pl.ds(part * columns, columns)], local_sems.at[2 + part]
        )
        for part in range(2)
    ]
    store_bottom = pltpu.make_async_copy(bottom, bottom_ref, local_sems.at[4])
    load_source.start()
    load_matrix.start()
    for load in load_fields:
        load.start()

    barrier = pltpu.get_barrier_semaphore()
    peers = [(section, flipped(member, t, members)) for t in range(1, members)]
    for step in (1, sections - 1):
        peers += [((section + step) % sections, flipped(member, t, members)) for t in range(members)]
    for peer in peers:
        pl.semaphore_signal(barrier, inc=1, device_id=peer, device_id_type=MESH)
    load_source.wait()

    @pl.when(top)
    def _():
        for part in range(2):
            adj[member, part] = staged[part].T

    with scope("bar"):
        pl.semaphore_wait(barrier, len(peers))

    def remote(src, dst, send_sem, recv_sem, to_section, to_member):
        return pltpu.make_async_remote_copy(
            src_ref=src,
            dst_ref=dst,
            send_sem=send_sem,
            recv_sem=recv_sem,
            device_id=(to_section, to_member),
            device_id_type=MESH,
        )

    def adj_view(m, held):
        return adj.at[held, :, sources_of(m), :]

    def fwd_view(m, held):
        return fwd.at[rows_of(held), :]

    def send_line(view, send, recv, m, finish=False, down=False):
        src = out_block.at[:, sources_of(m), :] if down else view(m, member)
        for t in range(outer):
            for u in range(inner if t == 0 else 1):
                if t == 0 and u == 0 and not down:
                    continue
                copy = remote(
                    src, view(m, member), send.at[m, t, u], recv.at[m, member], section - 1 if down else section, at(t, u)
                )
                condition = jnp.logical_not(crosses) if down and t == 0 and u > 0 else None
                guarded(condition, copy.wait_send if finish else copy.start)

    def arrival(view, recv, m, index):
        return remote(view(m, index), view(m, index), recv.at[m, index], recv.at[m, index], section, index)

    def forward(view, send, recv, m, t, finish=False):
        held = at(t, 0)
        for u in range(1, inner):
            copy = remote(view(m, held), view(m, held), send.at[m, t, u], recv.at[m, held], section, at(0, u))
            if finish:
                copy.wait_send()
            else:
                copy.start()

    def collect_line(view, send, recv, m, own_arrives=None, own_forward=None):
        if own_arrives is not None:
            pl.when(own_arrives)(arrival(view, recv, m, member).wait_recv)
        if own_forward is not None:
            pl.when(own_forward)(functools.partial(forward, view, send, recv, m, 0))
        for t in range(1, outer):
            arrival(view, recv, m, at(t, 0)).wait_recv()
            forward(view, send, recv, m, t)

    def finish_line(view, send, recv, m, own_forward=None):
        if own_forward is not None:
            pl.when(own_forward)(functools.partial(forward, view, send, recv, m, 0, finish=True))
        for t in range(1, outer):
            forward(view, send, recv, m, t, finish=True)

    def collect_inner(view, recv, m):
        for t in range(outer):
            for u in range(1, inner):
                arrival(view, recv, m, at(t, u)).wait_recv()

    lanes = min(128, harmonics)

    def build_onehots(whole):
        @pl.loop(0, harmonics // lanes)
        def _(index):
            start = pl.multiple_of(index * lanes, lanes)
            orders = orders_ref[...].reshape(1, harmonics)
            line = lax.broadcasted_iota(jnp.int32, (lanes, harmonics), 0)
            wanted = jnp.where(orders == start + line, 1.0, 0.0).astype(onehot_adj.dtype)
            onehot_adj[:, pl.ds(start, lanes)] = wanted.T

        @pl.loop(0, harmonics // block)
        def _(index):
            start = pl.multiple_of(index * block, block)
            orders = orders_ref[...].reshape(1, harmonics) - start
            if not whole:
                mine = orders[:, :rows]
                for m in range(1, members):
                    mine = jnp.where(member == m, orders[:, m * rows : (m + 1) * rows], mine)
                orders = mine
            size = orders.shape[1]
            line = lax.broadcasted_iota(jnp.int32, (block, size), 0)
            wanted = jnp.where(orders == block - 1 - line, 1.0, 0.0)
            onehot_fwd[pl.ds(start, block), :size] = wanted.astype(onehot_fwd.dtype)

        padded[:, :harmonics] = jnp.zeros((2 * columns, harmonics), padded.dtype)
        padded[:, 2 * harmonics :] = jnp.zeros((2 * columns, harmonics), padded.dtype)

    batch = math.gcd(4, harmonics // block)

    def sort_fields(whole):
        @pl.loop(0, harmonics // (block * batch))
        def _(index):
            here = pl.ds(pl.multiple_of(index * block * batch, block * batch), block * batch)
            if whole:
                sorted_rows = jnp.dot(onehot_fwd[here, :], fwd[...], preferred_element_type=jnp.float32)
            else:
                sorted_rows = jnp.dot(
                    onehot_fwd[here, :rows], fwd[rows_of(member), :], preferred_element_type=jnp.float32
                )
            for part in range(batch):
                piece = sorted_rows[part * block : (part + 1) * block]
                real, imag = piece[:, :columns], piece[:, columns:]
                place = index * batch + part
                left[place, :block, :] = jnp.concatenate([real, -imag], axis=1).astype(left.dtype)
                left[place, block:, :] = jnp.concatenate([imag, real], axis=1).astype(left.dtype)

    tile = math.gcd(512, harmonics)

    def sort_adjoint(helds, first):
        @pl.loop(0, harmonics // tile)
        def _(index):
            start = pl.multiple_of(index * tile, tile)
            here = pl.ds(pl.multiple_of(harmonics + start, tile), tile)
            total = None if first else padded[:, here].astype(jnp.float32)
            for held in helds:
                term = jnp.dot(
                    adj[held].reshape(2 * columns, rows),
                    onehot_adj[rows_of(held), pl.ds(start, tile)],
                    preferred_element_type=jnp.float32,
                )
                total = term if total is None else total + term
            padded[:, here] = total.astype(padded.dtype)

    def turn_matrix():
        deep = math.gcd(256, harmonics)

        @pl.loop(0, harmonics // deep)
        def _(index):
            here = pl.ds(pl.multiple_of(index * deep, deep), deep)
            for part in range(2):
                turned[part, here, :] = matrix[part, :, here].T

    @pl.when(top)
    def _():
        for m in range(chunks):
            send_line(adj_view, adj_send, adj_recv, m)

    for load in load_fields:
        load.wait()

    @pl.when(early)
    def _():
        send_line(fwd_view, fwd_send, fwd_recv, 0)

    load_matrix.wait()
    with scope("turn"):
        turn_matrix()

    def finish_fields():
        with scope("ef_finish"):
            collect_inner(fwd_view, fwd_recv, 0)
        with scope("ef_sort"):
            sort_fields(True)

    @pl.when(early)
    def _():
        with scope("ef_relay"):
            collect_line(fwd_view, fwd_forward, fwd_recv, 0)
        with scope("e_onehot"):
            build_onehots(True)

    @pl.when(section == 0)
    def _():
        finish_fields()

    @pl.when(jnp.logical_not(early) & jnp.logical_not(top))
    def _():
        with scope("l_onehot"):
            build_onehots(False)
        with scope("lf_sort"):
            sort_fields(False)

    own_forward = jnp.logical_not(crosses) & jnp.logical_not(top)
    near_blocks = [at(t, 0) for t in range(outer)]
    far_blocks = [at(t, u) for t in range(outer) for u in range(1, inner)]
    partials = {}

    def terms(m, helds):
        total = None
        for held in helds:
            real, imag = adj[held, 0, sources_of(m), :], adj[held, 1, sources_of(m), :]
            for part, values in enumerate(([real, imag], [-imag, real])):
                term = jnp.dot(
                    jnp.concatenate(values, axis=0),
                    turned[part, rows_of(held), :],
                    preferred_element_type=jnp.float32,
                )
                total = term if total is None else total + term
        return total

    def line_step(m):
        with scope("line%d" % m):
            collect_line(adj_view, adj_forward, adj_recv, m, jnp.logical_not(top), own_forward)

    def last_step(m):
        with scope("inner%d" % m):
            collect_inner(adj_view, adj_recv, m)
        total = partials[m] + terms(m, far_blocks)
        for part in range(2):
            out_block[part, sources_of(m), :] = total[part * span : (part + 1) * span].astype(out_block.dtype)

        @pl.when(section > 0)
        def _():
            send_line(adj_view, down_send, adj_recv, m, down=True)

    for m in range(chunks + AHEAD):
        if m < chunks:
            line_step(m)
        if m == chunks + AHEAD - 1:

            @pl.when(section == 0)
            def _():
                with scope("sort_near0"):
                    sort_adjoint(near_blocks, True)

        if m >= AHEAD:
            last_step(m - AHEAD)
        if m < chunks:
            partials[m] = terms(m, near_blocks)

    for part in range(2):
        bottom[part] = out_block[part].T
    store_bottom.start()

    @pl.when(top)
    def _():
        with scope("t_onehot"):
            build_onehots(False)
        with scope("t_sort"):
            sort_fields(False)

    @pl.when(early & (section > 0))
    def _():
        finish_fields()

    @pl.when(section > 0)
    def _():
        with scope("sort_near"):
            sort_adjoint(near_blocks, True)

    with scope("sort_far"):
        sort_adjoint(far_blocks, False)

    def diagonals(values, part):
        rolled = pltpu.roll(values[part * block : (part + 1) * block], width - block, 1, stride=1, stride_axis=0)
        return jnp.sum(rolled, axis=0, keepdims=True)[:, :band]

    @pl.when(early)
    def _():
        with scope("grad"):
            total = jnp.zeros((2 * block, width), jnp.float32)
            for index in range(harmonics // block):
                start = member * band + index * block
                if block % 128 == 0:
                    window = padded[:, pl.ds(pl.multiple_of(start, block), width)]
                else:
                    near_start = pl.multiple_of(start // 128 * 128, 128)
                    wide = padded[:, pl.ds(near_start, (width + 255) // 128 * 128)]
                    window = wide[:, :width]
                    for shift in range(block, 128, block):
                        window = jnp.where(start - near_start == shift, wide[:, shift : shift + width], window)
                total = total + jnp.dot(left[index], window, preferred_element_type=jnp.float32)
            for part in range(2):
                grads_ref[part : part + 1, :] = diagonals(total, part)

    step = math.gcd(256, 2 * harmonics)

    @pl.when(jnp.logical_not(early))
    def _():
        with scope("l_grad"):
            product[:, :block] = jnp.zeros((2 * block, block), jnp.float32)
            for first in range(0, 2 * harmonics, step):
                total = jnp.zeros((2 * block, step), jnp.float32)
                for index in range(harmonics // block):
                    start = first + block * (index + 1) - harmonics
                    if start + step > 0 and start < harmonics:
                        window = padded[:, harmonics + start : harmonics + start + step]
                        total = total + jnp.dot(left[index], window, preferred_element_type=jnp.float32)
                product[:, block + first : block + first + step] = total
        with scope("l_diag"):
            for m in range(members):
                values = product[:, m * band : m * band + width]
                for part in range(2):
                    partial[m, part : part + 1, :] = diagonals(values, part)

        def sums(t):
            to = flipped(member, t, members)
            return remote(partial.at[to], arrived.at[member], sum_send.at[t], sum_recv.at[member], section, to)

        with scope("l_sum"):
            for t in range(1, members):
                sums(t).start()
            total = partial[member]
            for t in range(1, members):
                other = flipped(member, t, members)
                remote(
                    arrived.at[other], arrived.at[other], sum_recv.at[other], sum_recv.at[other], section, other
                ).wait_recv()
                total = total + arrived[other]
            grads_ref[...] = total
            for t in range(1, members):
                sums(t).wait_send()

    with scope("fin"):
        store_bottom.wait()
        for m in range(chunks):
            finish_line(adj_view, adj_forward, adj_recv, m, own_forward)

        @pl.when(early)
        def _():
            send_line(fwd_view, fwd_send, fwd_recv, 0, finish=True)
            finish_line(fwd_view, fwd_forward, fwd_recv, 0)

        @pl.when(top)
        def _():
            for m in range(chunks):
                send_line(adj_view, adj_send, adj_recv, m, finish=True)

        @pl.when(section > 0)
        def _():
            for m in range(chunks):
                send_line(adj_view, down_send, adj_recv, m, finish=True, down=True)


def per_device(source, transfer, fields, orders):
    harmonics = orders.shape[0]
    sections = lax.axis_size("layer")
    members = lax.axis_size("harm")
    rows = transfer.shape[2]
    columns = source.shape[2]
    inner = 1 << ((members.bit_length() - 1) // 2)
    outer = members // inner
    band = 2 * harmonics // members
    block = min(128, band)
    chunks = math.gcd(CHUNKS, columns)
    norm_scale = 1.0 / math.sqrt(harmonics * columns)
    any_space = pl.BlockSpec(memory_space=pl.ANY)
    vmem = pl.BlockSpec(memory_space=pltpu.VMEM)
    dma = pltpu.SemaphoreType.DMA
    grads, bottom = pl.pallas_call(
        functools.partial(sweep_kernel, sections, members, inner, block),
        out_shape=(
            jax.ShapeDtypeStruct((2, band), jnp.float32),
            jax.ShapeDtypeStruct((2, rows, columns), jnp.bfloat16),
        ),
        in_specs=[any_space, any_space, any_space, vmem],
        out_specs=(vmem, any_space),
        scratch_shapes=[
            pltpu.VMEM((2, rows, harmonics), jnp.bfloat16),
            pltpu.VMEM((2, harmonics, rows), jnp.bfloat16),
            pltpu.VMEM((2, rows, columns), jnp.bfloat16),
            pltpu.VMEM((members, 2, columns, rows), jnp.bfloat16),
            pltpu.VMEM((harmonics, 2 * columns), jnp.bfloat16),
            pltpu.VMEM((2, columns, rows), jnp.bfloat16),
            pltpu.VMEM((2, rows, columns), jnp.bfloat16),
            pltpu.VMEM((harmonics, harmonics), jnp.bfloat16),
            pltpu.VMEM((harmonics, harmonics), jnp.bfloat16),
            pltpu.VMEM((harmonics // block, 2 * block, 2 * columns), jnp.bfloat16),
            pltpu.VMEM((2 * columns, 3 * harmonics), jnp.bfloat16),
            pltpu.VMEM((2 * block, block + 2 * harmonics), jnp.float32),
            pltpu.VMEM((members, 2, band), jnp.float32),
            pltpu.VMEM((members, 2, band), jnp.float32),
            dma((5,)),
            dma((chunks, members)),
            dma((chunks, outer, inner)),
            dma((chunks, outer, inner)),
            dma((chunks, outer, inner)),
            dma((1, members)),
            dma((1, outer, inner)),
            dma((1, outer, inner)),
            dma((members,)),
            dma((members,)),
        ],
        compiler_params=pltpu.CompilerParams(collective_id=0, has_side_effects=True),
        name="sweep",
    )(source, transfer, fields, orders)
    return (grads * norm_scale)[None], bottom[None]


def solution(mesh):
    return jax.shard_map(
        per_device,
        mesh=mesh,
        in_specs=(
            P(None, "harm", None),
            P("layer", None, "harm", None),
            P("layer", None, "harm", None),
            P(),
        ),
        out_specs=(P("layer", None, "harm"), P("layer", None, "harm", None)),
        check_vma=False,
    )
```

time: 61 us -> 51.1 us (0.84)
  Pallas kernels: 57.3 us -> 47.4 us
    pallas_call x1, Pallas kernels: 57.3 us -> 47.4 us  [per_device(): pl.pallas_call(functools.partial(sweep_kernel, sections, members, inner,...]
where the time goes in v2:
time: 51.1 us; the launch traced here: 50.9 us
  Pallas kernels  47.4 us (93%)
  local copies, waits for them, and re-layouts  1.57 us (3%)
  other arithmetic  1.28 us (3%)
  between operations  0.64 us (1%)
    pallas_call x1, Pallas kernels, per_device(): pl.pallas_call(functools.partial(sweep_kernel, sections, members, inner,...  47.4 us
    unnamed x1, local copies, waits for them, and re-layouts  1.57 us
    broadcast_in_dim x1, other arithmetic, per_device(): return ((grads * norm_scale)[None], bottom[None])  1.28 us

profile of v2, /device:TPU:0, one launch (start us, length us, event | category | flops | bytes accessed | tf_op | source)
XLA Modules:
  0.0 50.9 jit_solution(18312449753540855962)
XLA Ops:
  0.6 47.4 %sweep.1 = (f32[2,512]{1,0:T(2,128)}, bf16[2,256,128]{2,1,0:T(8,128)(2,1)}) custom-call(bf16[2,256,128]{2,1,0:T(8,128)(2,1)} %source_ref.1, bf16[1,2,256,2048]{3,2,1,0:T(8,128)(2,1)} %transfer_ref.1, bf16[1,2,256,128]{3,2,1,0:T(8,128)(2,1)} %fields_ref.1, s32[2048]{0:T(1024)} %orders_ref.1), custom_call_target="tpu_custom_call" | custom-call | tf_op jit(solution)/shard_map/sweep/pallas_call | solution.py:467
  48.0 1.3 %multiply_bitcast_fusion = f32[1,2,512]{2,1,0:T(2,128)} fusion(f32[2,512]{1,0:T(2,128)} %get-tuple-element.4), kind=kLoop, calls=%fused_computation | loop fusion | flops 1024 | bytes 8192 | tf_op jit(solution)/shard_map/broadcast_in_dim | solution.py:504
  49.3 1.6 %copy.7 = bf16[1,2,256,128]{3,2,1,0:T(8,128)(2,1)} copy(bf16[1,2,256,128]{3,2,1,0:T(8,128)(2,1)} %bitcast.3) | data formatting | bytes 262144
